TPU v7x, 32 devices: a whole 2x2x4 slice. The times are simulated.
32 devices in a mesh: grp: 4 (over y, x), row: 8 (over z, core).
Axes of the slice: x: 2, y: 2, z: 4, core: 2. Of those that a mesh axis runs over, the one named last changes fastest.
Arguments:
- blocks: bfloat16 [32, 4, 10, 256, 256], P(('grp', 'row')), may hold values from 0 to 1
- columns: int32 [32, 4, 10], P(('grp', 'row')), may hold values from -1 to 31, as said below
- factor: bfloat16 [64, 8192], P(None, ('grp', 'row')), may hold values from 0 to 0.3, as said below
Outputs:
- updated: float32 [64, 8192], P(None, ('grp', 'row'))
Inputs may be any that keep to these rules, and one draw needn't show every extreme that they name: Tile row i lies in group g = i // 8. In block h of tile row i the live slots come first and name distinct tile columns of group h (h * 8 to h * 8 + 7), none above i; block g always names i itself; blocks h > g are empty; a block holds at most 10 live slots, and -1 marks an empty slot. `factor`: entries are nonnegative.
All inputs are finite; a program needn't handle non-finite values.
Results may differ from a plain program's by a relative error of at most 0.0003.
Values may be sent and summed in bfloat16 or wider, within the bound.
No kernel may reach another device: no remote copies, remote signals or barrier semaphores. Data moves between devices by JAX's collectives and lax.ppermute only.
A program may use at most 128 MiB of HBM per device.

v0:
```python
import jax
import jax.numpy as jnp
from jax import lax
from jax.sharding import PartitionSpec as P

floor_value = 1e-06


def sweep(current, products, gram):

    def update(column, current):
        weights = lax.dynamic_index_in_dim(gram, column, 1, keepdims=False)
        fitted = jnp.dot(weights, current, precision=lax.Precision.HIGHEST)
        target = lax.dynamic_index_in_dim(products, column, 0, keepdims=False)
        present = lax.dynamic_index_in_dim(current, column, 0, keepdims=False)
        diagonal = gram[column, column]
        fresh = jnp.maximum(present + (target - fitted) / diagonal, floor_value)
        return lax.dynamic_update_index_in_dim(current, fresh, column, 0)

    return lax.fori_loop(0, current.shape[0], update, current)


def choose_rows(group_cols, group_number, rows_grp):
    offsets = group_cols - group_number * rows_grp
    positions = lax.broadcasted_iota(jnp.int32, (group_cols.shape[0], rows_grp), 1)
    return (offsets[:, None] == positions) & (group_cols >= 0)[:, None]


def lower_work(group_tiles, group_cols, group_number, group_factor, rows_grp):
    rank_count, span = group_factor.shape
    tile_size = span // rows_grp
    stacked = group_factor.reshape(rank_count, rows_grp, tile_size)
    selected = choose_rows(group_cols, group_number, rows_grp)
    fetched = jnp.einsum(
        "sn,rnt->srt", selected.astype(jnp.bfloat16), stacked, preferred_element_type=jnp.float32
    ).astype(jnp.bfloat16)
    return jnp.einsum("srv,suv->ru", fetched, group_tiles, preferred_element_type=jnp.float32)


def per_device(blocks, columns, factor):
    tiles_dev = blocks[0]
    cols_dev = columns[0]
    rank_count, tile_size = factor.shape
    rows_grp = lax.axis_size("row")
    group_count = lax.axis_size("grp")
    span = rows_grp * tile_size
    gram = lax.psum(jnp.dot(factor, factor.T, preferred_element_type=jnp.float32), ("grp", "row"))
    group_factor = lax.all_gather(factor, "row", axis=1, tiled=True)
    my_group = lax.axis_index("grp")
    slot_count = cols_dev.shape[1]
    live = (cols_dev >= 0).astype(jnp.float32)
    mirror = jnp.einsum("ru,hsuv->hsrv", factor, tiles_dev, preferred_element_type=jnp.float32)
    mirror = mirror * live[:, :, None, None]
    arrived, arrived_cols = (
        lax.all_to_all(mirror, "grp", split_axis=0, concat_axis=0, tiled=True),
        lax.all_to_all(cols_dev, "grp", split_axis=0, concat_axis=0, tiled=True),
    )
    flat_cols = arrived_cols.reshape(group_count * slot_count)
    selected = choose_rows(flat_cols, my_group, rows_grp).astype(jnp.float32)
    flat_mirror = arrived.reshape(group_count * slot_count, rank_count, tile_size)
    spread = jnp.einsum("sn,srv->rnv", selected, flat_mirror, precision=lax.Precision.HIGHEST)
    mirror_sum = lax.psum_scatter(
        spread.reshape(rank_count, span), "row", scatter_dimension=1, tiled=True
    )
    lower_sum = jnp.zeros((rank_count, tile_size), jnp.float32)
    piece = lax.all_gather(group_factor, "grp", axis=1, tiled=True)
    begin_at = jnp.int32(0)
    for offset in range(piece.shape[1] // span):
        group_number = begin_at // span + offset
        group_tiles = lax.dynamic_index_in_dim(tiles_dev, group_number, 0, keepdims=False)
        group_cols = lax.dynamic_index_in_dim(cols_dev, group_number, 0, keepdims=False)
        block_cols = lax.dynamic_slice_in_dim(piece, offset * span, span, 1)
        lower_sum = lower_sum + lower_work(
            group_tiles, group_cols, group_number, block_cols, rows_grp
        )
    products = lower_sum + mirror_sum
    return sweep(factor.astype(jnp.float32), products, gram)


def solution(mesh):
    in_specs = (
        P(("grp", "row"), None, None, None, None),
        P(("grp", "row"), None, None),
        P(None, ("grp", "row")),
    )
    out_specs = P(None, ("grp", "row"))
    return jax.shard_map(
        per_device, mesh=mesh, in_specs=in_specs, out_specs=out_specs, check_vma=False
    )
```

profile of v0, /device:TPU:0, one launch (start us, length us, event | category | flops | bytes accessed | tf_op | source)
XLA Modules:
  0.0 246.8 jit_solution(16195418602525848965)
XLA Ops:
  7.4 5.2 %all-to-all-start.1 = ((s32[4,1,10]{2,1,0:T(1,128)}), s32[4,1,10]{2,1,0:T(1,128)S(1)}, u32[]{:S(2)}, u32[]{:S(2)}) async-start(s32[4,1,10]{2,1,0:T(1,128)} %bitcast.144), calls=%async_computation.1 | async-start | bytes 4096 | tf_op jit(solution)/shard_map/all_to_all | solution.py:56
  12.6 15.7 %all_gather.6 = bf16[64,2048]{1,0:T(8,128)(2,1)} all-gather(bf16[64,256]{1,0:T(8,128)(2,1)} %param.7), channel_id=1, replica_groups=mesh['grp'=4,'row'=8] {'row'}, dimensions={1}, use_global_device_ids=true | all-gather | bytes 294912 | tf_op jit(solution)/shard_map/all_gather | solution.py:48
  28.3 0.7 convert_bitcast_fusion
  29.0 5.1 %multiply_bitcast_fusion = f32[4,10,64,256]{3,2,1,0:T(8,128)} fusion(bf16[1,4,10,256,256]{4,3,2,1,0:T(8,128)(2,1)} %param.5, f32[4,10]{1,0:T(4,128)S(1)} %convert_bitcast_fusion, bf16[64,256]{1,0:T(8,128)(2,1)} %param.7), kind=kOutput, calls=%fused_computation.10 | convolution fusion | flops 336199680 | bytes 7897248 | tf_op jit(solution)/shard_map/ru,hsuv->hsrv/dot_general | solution.py:52
  34.1 4.4 %all-to-all-start = ((f32[4,10,64,256]{3,2,1,0:T(8,128)}), f32[4,10,64,256]{3,2,1,0:T(8,128)S(1)}, u32[]{:S(2)}, u32[]{:S(2)}) async-start(f32[4,10,64,256]{3,2,1,0:T(8,128)} %multiply_bitcast_fusion), calls=%async_computation | async-start | bytes 5242880 | tf_op jit(solution)/shard_map/all_to_all | solution.py:55
  38.6 71.8 %psum.7 = f32[64,64]{1,0:T(8,128)S(1)} all-reduce(f32[64,64]{1,0:T(8,128)S(1)} %fusion.75), channel_id=1, replica_groups=mesh['grp'=4,'row'=8] {'grp','row'}, use_global_device_ids=true, to_apply=%region_0.0 | all-reduce | flops 4096 | bytes 32768 | tf_op jit(solution)/shard_map/psum | solution.py:47
  110.8 1.3 fusion.74
  112.2 1.2 convolution_convert_fusion.3
  113.3 1.1 convolution_convert_fusion.2
  114.5 2.4 fusion.4
  116.9 1.0 copy.21
  117.9 2.0 fusion.20
  120.7 1.8 fusion.41
  122.5 1.8 fusion.38
  124.4 24.2 %reduce-scatter.2.cloned.1.call-done = f32[64,256]{1,0:T(8,128)} async-done(((f32[64,2048]{1,0:T(8,128)}), f32[64,256]{1,0:T(8,128)}) %reduce-scatter.2.cloned.1.call-update) | async-done | bytes 65552 | tf_op jit(solution)/shard_map/reduce_scatter | solution.py:62
  148.6 1.8 fusion.35
  150.4 88.3 %while.13 = (s32[]{:T(128)}, f32[64,256]{1,0:T(8,128)S(1)}, f32[64,256]{1,0:T(8,128)S(1)}, f32[64,64]{0,1:T(8,128)S(1)}, s32[]{:T(128)}, /*index=5*/s32[]{:T(128)}) while((s32[]{:T(128)}, f32[64,256]{1,0:T(8,128)S(1)}, f32[64,256]{1,0:T(8,128)S(1)}, f32[64,64]{0,1:T(8,128)S(1)}, s32[]{:T(128)}, /*index=5*/s32[]{:T(128)}) %tuple.42), condition=%wide.region_3.4_spmd, body=%wide.region_2.3_spmd.sunk | while | flops 197634 | bytes 77417 | solution.py:20
  150.6 0.6 dynamic_slice.138
  151.9 0.6 dynamic_slice.138
  153.3 0.6 dynamic_slice.138
  154.7 0.6 dynamic_slice.138
  156.1 0.6 dynamic_slice.138
  157.5 0.6 dynamic_slice.138
  158.8 0.6 dynamic_slice.138
  160.2 0.6 dynamic_slice.138
  161.6 0.6 dynamic_slice.138
  163.0 0.6 dynamic_slice.138
  164.4 0.6 dynamic_slice.138
  165.7 0.6 dynamic_slice.138
  167.1 0.6 dynamic_slice.138
  168.5 0.6 dynamic_slice.138
  169.9 0.6 dynamic_slice.138
  171.3 0.6 dynamic_slice.138
  172.6 0.6 dynamic_slice.138
  174.0 0.6 dynamic_slice.138
  175.4 0.6 dynamic_slice.138
  176.8 0.6 dynamic_slice.138
  178.2 0.6 dynamic_slice.138
  179.5 0.6 dynamic_slice.138
  180.9 0.6 dynamic_slice.138
  182.3 0.6 dynamic_slice.138
  183.7 0.6 dynamic_slice.138
  185.1 0.6 dynamic_slice.138
  186.4 0.6 dynamic_slice.138
  187.8 0.6 dynamic_slice.138
  189.2 0.6 dynamic_slice.138
  190.6 0.6 dynamic_slice.138
  238.7 0.6 copy-done
  (320 shorter events, 69.9 us)
Async XLA Ops:
  7.4 26.7 %all-to-all-start.1 = ((s32[4,1,10]{2,1,0:T(1,128)}), s32[4,1,10]{2,1,0:T(1,128)S(1)}, u32[]{:S(2)}, u32[]{:S(2)}) async-start(s32[4,1,10]{2,1,0:T(1,128)} %bitcast.144), calls=%async_computation.1 | async-start | bytes 4096 | tf_op jit(solution)/shard_map/all_to_all | solution.py:56
  12.6 98.2 %all-gather.2.cloned.1.call-start = ((), (), s32[]{:S(2)}) async-start(), calls=%async_computation.3 | async-start | bytes 1310720 | tf_op jit(solution)/shard_map/all_gather | solution.py:66
  34.0 4.4 %copy-start.1 = (bf16[64,256]{1,0:T(8,128)(2,1)S(1)}, bf16[64,256]{1,0:T(8,128)(2,1)}, u32[]{:S(2)}) copy-start(bf16[64,256]{1,0:T(8,128)(2,1)} %param.7) | copy-start | bytes 98308
  34.0 76.4 %copy-start.3 = (s32[1,4,10]{2,1,0:T(4,128)S(1)}, s32[1,4,10]{2,1,0:T(4,128)}, u32[]{:S(2)}) copy-start(s32[1,4,10]{2,1,0:T(4,128)} %param.6) | copy-start | bytes 484
  34.1 80.4 %all-to-all-start = ((f32[4,10,64,256]{3,2,1,0:T(8,128)}), f32[4,10,64,256]{3,2,1,0:T(8,128)S(1)}, u32[]{:S(2)}, u32[]{:S(2)}) async-start(f32[4,10,64,256]{3,2,1,0:T(8,128)} %multiply_bitcast_fusion), calls=%async_computation | async-start | bytes 5242880 | tf_op jit(solution)/shard_map/all_to_all | solution.py:55
  38.4 110.1 %reduce-scatter.2.cloned.1.call-start = ((), (), s32[]{:S(2)}) async-start(), calls=%async_computation.4 | async-start | bytes 589824 | tf_op jit(solution)/shard_map/reduce_scatter | solution.py:62
  117.8 2.9 %copy-start.2 = (bf16[10,64,256]{2,0,1:T(8,128)(2,1)S(1)}, bf16[10,64,256]{2,0,1:T(8,128)(2,1)}, u32[]{:S(2)}) copy-start(bf16[10,64,256]{2,0,1:T(8,128)(2,1)} %convolution_convert_fusion.2) | copy-start | bytes 983044
  238.7 0.6 copy-start
Sparse Core Ops, SparseCore 0:
  28.4 48.7 all-gather.1
Sparse Core Ops, SparseCore 1:
  117.9 30.6 reduce-scatter.1
where the time goes:
time: 248 us; the launch traced here: 247 us
  blocking collectives  87.5 us (35%)
  local copies, waits for them, and re-layouts  44.1 us (18%)
  other arithmetic  36.8 us (15%)
  matrix products  27.2 us (11%)
  waiting for transfers between devices  24.2 us (10%)
  between operations  15 us (6%)
  starting transfers between devices  9.57 us (4%)
    psum x1, blocking collectives, per_device(): lax.psum(jnp.dot(factor, factor.T, preferred_element_type=jnp.float32), (...  71.8 us
    dynamic_slice x64, local copies, waits for them, and re-layouts, update(): diagonal = gram[column, column]  37.4 us
    max x64, other arithmetic, update(): fresh = jnp.maximum(present + (target - fitted) / diagonal, floor_value)  36.1 us
    reduce_scatter x1, waiting for transfers between devices, per_device(): lax.psum_scatter(spread.reshape(rank_count, span), 'row', scatter_dimensi...  24.2 us
    all_gather x1, blocking collectives, per_device(): group_factor = lax.all_gather(factor, 'row', axis=1, tiled=True)  15.7 us
    dot_general x64, matrix products, update(): fitted = jnp.dot(weights, current, precision=lax.Precision.HIGHEST)  9.16 us
    dot_general x4, matrix products, lower_work(): jnp.einsum('srv,suv->ru', fetched, group_tiles, preferred_element_type=jn...  7.5 us
    all_to_all x1, starting transfers between devices, per_device(): lax.all_to_all(cols_dev, 'grp', split_axis=0, concat_axis=0, tiled=True)  5.19 us
  transfers between devices with their start and end apart: 4, of which 1 were waited for; matrix products, arithmetic and copies ran while one was open for 7% of the time, Pallas kernels for 0%

commit v1 on v0

--- a/solution.py
+++ b/solution.py
@@ -44,7 +44,9 @@
     rows_grp = lax.axis_size("row")
     group_count = lax.axis_size("grp")
     span = rows_grp * tile_size
-    gram = lax.psum(jnp.dot(factor, factor.T, preferred_element_type=jnp.float32), ("grp", "row"))
+    gram = lax.psum(
+        lax.psum(jnp.dot(factor, factor.T, preferred_element_type=jnp.float32), "row"), "grp"
+    )
     group_factor = lax.all_gather(factor, "row", axis=1, tiled=True)
     my_group = lax.axis_index("grp")
     slot_count = cols_dev.shape[1]

time: 248 us -> 229 us (0.923)
  blocking collectives: 87.5 us -> 63.5 us
  other arithmetic: 36.8 us -> 40.6 us
    psum x1 -> x2, blocking collectives: 71.8 us -> 47.7 us  [the longest x1 28.8 us: per_device(): lax.psum(jnp.dot(factor, factor.T, preferred_element_type=jnp.float32), '...]
    max x64, other arithmetic: 36.1 us -> 39.8 us  [update(): fresh = jnp.maximum(present + (target - fitted) / diagonal, floor_value)]
where the time goes in v1:
time: 229 us; the launch traced here: 228 us
  blocking collectives  63.5 us (28%)
  local copies, waits for them, and re-layouts  45.1 us (20%)
  other arithmetic  40.6 us (18%)
  matrix products  27.2 us (12%)
  waiting for transfers between devices  24.8 us (11%)
  between operations  15 us (7%)
  starting transfers between devices  9.57 us (4%)
  loops' own time  2.29 us (1%)
    max x64, other arithmetic, update(): fresh = jnp.maximum(present + (target - fitted) / diagonal, floor_value)  39.8 us
    dynamic_slice x64, local copies, waits for them, and re-layouts, update(): diagonal = gram[column, column]  38.4 us
    psum x1, blocking collectives, per_device(): lax.psum(jnp.dot(factor, factor.T, preferred_element_type=jnp.float32), '...  28.8 us
    reduce_scatter x1, waiting for transfers between devices, per_device(): lax.psum_scatter(spread.reshape(rank_count, span), 'row', scatter_dimensi...  24.8 us
    psum x1, blocking collectives, per_device(): lax.psum(lax.psum(jnp.dot(factor, factor.T, preferred_element_type=jnp.fl...  18.9 us
    all_gather x1, blocking collectives, per_device(): group_factor = lax.all_gather(factor, 'row', axis=1, tiled=True)  15.7 us
    dot_general x64, matrix products, update(): fitted = jnp.dot(weights, current, precision=lax.Precision.HIGHEST)  9.16 us
    dot_general x4, matrix products, lower_work(): jnp.einsum('srv,suv->ru', fetched, group_tiles, preferred_element_type=jn...  7.48 us
  transfers between devices with their start and end apart: 4, of which 1 were waited for; matrix products, arithmetic and copies ran while one was open for 7% of the time, Pallas kernels for 0%

profile of v1, /device:TPU:0, one launch (start us, length us, event | category | flops | bytes accessed | tf_op | source)
XLA Modules:
  0.0 228.1 jit_solution(4863688492358381266)
XLA Ops:
  7.4 5.2 %all-to-all-start.1 = ((s32[4,1,10]{2,1,0:T(1,128)}), s32[4,1,10]{2,1,0:T(1,128)S(1)}, u32[]{:S(2)}, u32[]{:S(2)}) async-start(s32[4,1,10]{2,1,0:T(1,128)} %bitcast.144), calls=%async_computation.1 | async-start | bytes 4096 | tf_op jit(solution)/shard_map/all_to_all | solution.py:58
  12.6 15.7 %all_gather.6 = bf16[64,2048]{1,0:T(8,128)(2,1)} all-gather(bf16[64,256]{1,0:T(8,128)(2,1)} %param.7), channel_id=1, replica_groups=mesh['grp'=4,'row'=8] {'row'}, dimensions={1}, use_global_device_ids=true | all-gather | bytes 294912 | tf_op jit(solution)/shard_map/all_gather | solution.py:50
  28.3 0.7 convert_bitcast_fusion
  29.0 5.0 %multiply_bitcast_fusion = f32[4,10,64,256]{3,2,1,0:T(8,128)} fusion(bf16[1,4,10,256,256]{4,3,2,1,0:T(8,128)(2,1)} %param.5, f32[4,10]{1,0:T(4,128)S(1)} %convert_bitcast_fusion, bf16[64,256]{1,0:T(8,128)(2,1)} %param.7), kind=kOutput, calls=%fused_computation.10 | convolution fusion | flops 336199680 | bytes 7897248 | tf_op jit(solution)/shard_map/ru,hsuv->hsrv/dot_general | solution.py:54
  34.0 4.4 %all-to-all-start = ((f32[4,10,64,256]{3,2,1,0:T(8,128)}), f32[4,10,64,256]{3,2,1,0:T(8,128)S(1)}, u32[]{:S(2)}, u32[]{:S(2)}) async-start(f32[4,10,64,256]{3,2,1,0:T(8,128)} %multiply_bitcast_fusion), calls=%async_computation | async-start | bytes 5242880 | tf_op jit(solution)/shard_map/all_to_all | solution.py:57
  38.6 28.8 %psum.14 = f32[64,64]{1,0:T(8,128)S(1)} all-reduce(f32[64,64]{1,0:T(8,128)S(1)} %fusion.75), channel_id=1, replica_groups=mesh['grp'=4,'row'=8] {'row'}, use_global_device_ids=true, to_apply=%region_0.0 | all-reduce | flops 4096 | bytes 32768 | tf_op jit(solution)/shard_map/psum | solution.py:48
  67.4 18.9 %psum.15 = f32[64,64]{1,0:T(8,128)S(1)} all-reduce(f32[64,64]{1,0:T(8,128)S(1)} %psum.14), channel_id=1, replica_groups=mesh['grp'=4,'row'=8] {'grp'}, use_global_device_ids=true, to_apply=%region_1.0 | all-reduce | flops 4096 | bytes 32768 | tf_op jit(solution)/shard_map/psum | solution.py:47
  86.6 1.3 fusion.74
  88.1 1.2 convolution_convert_fusion.3
  89.2 1.1 convolution_convert_fusion.2
  90.4 2.4 %fusion.4 = f32[64,256,8]{1,2,0:T(8,128)S(1)} fusion(f32[40,64,256]{2,1,0:T(8,128)S(1)} %bitcast.129, s32[40]{0:T(128)S(1)} %sub.63, pred[40]{0:T(512)(128)(4,1)S(1)} %ge.72), kind=kOutput, calls=%fused_computation.8 | convolution fusion | flops 62915200 | bytes 3145928 | tf_op jit(solution)/shard_map/sn,srv->rnv/dot_general | solution.py:63
  92.8 1.0 copy.21
  93.8 2.0 fusion.20
  96.6 1.8 fusion.41
  98.4 1.8 fusion.38
  100.3 24.8 %reduce-scatter.2.cloned.1.call-done = f32[64,256]{1,0:T(8,128)} async-done(((f32[64,2048]{1,0:T(8,128)}), f32[64,256]{1,0:T(8,128)}) %reduce-scatter.2.cloned.1.call-update) | async-done | bytes 65552 | tf_op jit(solution)/shard_map/reduce_scatter | solution.py:64
  125.1 1.8 fusion.35
  126.9 93.1 %while.13 = (s32[]{:T(128)}, f32[64,256]{1,0:T(8,128)S(1)}, f32[64,256]{1,0:T(8,128)S(1)}, f32[64,64]{0,1:T(8,128)S(1)}, s32[]{:T(128)}, /*index=5*/s32[]{:T(128)}) while((s32[]{:T(128)}, f32[64,256]{1,0:T(8,128)S(1)}, f32[64,256]{1,0:T(8,128)S(1)}, f32[64,64]{0,1:T(8,128)S(1)}, s32[]{:T(128)}, /*index=5*/s32[]{:T(128)}) %tuple.42), condition=%wide.region_4.5_spmd, body=%wide.region_3.4_spmd.sunk | while | flops 197634 | bytes 77417 | solution.py:20
  127.7 0.6 fusion.88
  129.1 0.6 fusion.88
  130.6 0.6 fusion.88
  136.4 0.6 fusion.88
  137.8 0.6 fusion.88
  139.3 0.6 fusion.88
  140.7 0.6 fusion.88
  145.1 0.6 fusion.88
  146.6 0.6 fusion.88
  148.0 0.6 fusion.88
  149.5 0.6 fusion.88
  155.3 0.6 fusion.88
  156.7 0.6 fusion.88
  158.2 0.6 fusion.88
  164.0 0.6 fusion.88
  165.5 0.6 fusion.88
  166.9 0.6 fusion.88
  168.4 0.6 fusion.88
  172.8 0.6 fusion.88
  174.2 0.6 fusion.88
  175.7 0.6 fusion.88
  177.1 0.6 fusion.88
  182.9 0.6 fusion.88
  184.4 0.6 fusion.88
  185.8 0.6 fusion.88
  191.7 0.6 fusion.88
  193.1 0.6 fusion.88
  194.6 0.6 fusion.88
  196.0 0.6 fusion.88
  200.4 0.6 fusion.88
  (321 shorter events, 74.2 us)
Async XLA Ops:
  7.4 26.7 %all-to-all-start.1 = ((s32[4,1,10]{2,1,0:T(1,128)}), s32[4,1,10]{2,1,0:T(1,128)S(1)}, u32[]{:S(2)}, u32[]{:S(2)}) async-start(s32[4,1,10]{2,1,0:T(1,128)} %bitcast.144), calls=%async_computation.1 | async-start | bytes 4096 | tf_op jit(solution)/shard_map/all_to_all | solution.py:58
  12.6 74.1 %all-gather.2.cloned.1.call-start = ((), (), s32[]{:S(2)}) async-start(), calls=%async_computation.3 | async-start | bytes 1310720 | tf_op jit(solution)/shard_map/all_gather | solution.py:68
  34.0 4.4 %copy-start.1 = (bf16[64,256]{1,0:T(8,128)(2,1)S(1)}, bf16[64,256]{1,0:T(8,128)(2,1)}, u32[]{:S(2)}) copy-start(bf16[64,256]{1,0:T(8,128)(2,1)} %param.7) | copy-start | bytes 98308
  34.0 52.4 %copy-start.3 = (s32[1,4,10]{2,1,0:T(4,128)S(1)}, s32[1,4,10]{2,1,0:T(4,128)}, u32[]{:S(2)}) copy-start(s32[1,4,10]{2,1,0:T(4,128)} %param.6) | copy-start | bytes 484
  34.0 56.3 %all-to-all-start = ((f32[4,10,64,256]{3,2,1,0:T(8,128)}), f32[4,10,64,256]{3,2,1,0:T(8,128)S(1)}, u32[]{:S(2)}, u32[]{:S(2)}) async-start(f32[4,10,64,256]{3,2,1,0:T(8,128)} %multiply_bitcast_fusion), calls=%async_computation | async-start | bytes 5242880 | tf_op jit(solution)/shard_map/all_to_all | solution.py:57
  38.4 86.7 %reduce-scatter.2.cloned.1.call-start = ((), (), s32[]{:S(2)}) async-start(), calls=%async_computation.4 | async-start | bytes 589824 | tf_op jit(solution)/shard_map/reduce_scatter | solution.py:64
  93.7 2.9 %copy-start.2 = (bf16[10,64,256]{2,0,1:T(8,128)(2,1)S(1)}, bf16[10,64,256]{2,0,1:T(8,128)(2,1)}, u32[]{:S(2)}) copy-start(bf16[10,64,256]{2,0,1:T(8,128)(2,1)} %convolution_convert_fusion.2) | copy-start | bytes 983044
  220.0 0.6 copy-start
Sparse Core Ops, SparseCore 0:
  28.4 48.7 all-gather.1
Sparse Core Ops, SparseCore 1:
  93.8 31.2 reduce-scatter.1
